TPU v7x, 32 devices: a whole 2x2x4 slice. The times are simulated.
32 devices in a mesh: gx: 4 (over y, x), gy: 2 (over core), gz: 4 (over z).
Axes of the slice: x: 2, y: 2, z: 4, core: 2. Of those that a mesh axis runs over, the one named last changes fastest.
Arguments:
- rhs: float32 [8, 64, 64, 512], P(None, 'gx', 'gy', 'gz'), may hold values from -8 to 8
- stencil: float32 [14, 64, 64, 512], P(None, 'gx', 'gy', 'gz'), may hold values from 0.02 to 1
Outputs:
- solution: float32 [8, 64, 64, 512], P(None, 'gx', 'gy', 'gz')
- residual: float32 [8, 64, 64, 512], P(None, 'gx', 'gy', 'gz')
All inputs are finite; a program needn't handle non-finite values.
Results may differ from a plain program's by a relative error of at most 0.00029.
Values sent between devices are 32-bit elements; how exact they have to be, the bound alone decides.
A program may use at most 128 MiB of HBM per device.

v0:
```python
import jax
import jax.numpy as jnp
from jax import lax
from jax.sharding import PartitionSpec as P

ITERS = 2
FORWARD = [
    (a, b, c) for a in (-1, 0, 1) for b in (-1, 0, 1) for c in (-1, 0, 1) if (a, b, c) > (0, 0, 0)
]


def with_halo(cells, sides, width):
    for axis, dim in sides:
        count = lax.axis_size(axis)
        ends = count - 1
        head = lax.slice_in_dim(cells, 0, width, axis=dim)
        tail = lax.slice_in_dim(cells, cells.shape[dim] - width, cells.shape[dim], axis=dim)
        cells = jnp.concatenate(
            [
                lax.ppermute(tail, axis, [(i, (i + 1) % count) for i in range(ends)]),
                cells,
                lax.ppermute(head, axis, [((i + 1) % count, i) for i in range(ends)]),
            ],
            axis=dim,
        )
    return cells


def window(array, margin, depth, offset):
    result = array
    for place in range(3):
        dim = array.ndim - 3 + place
        inner = array.shape[dim] - 2 * margin
        begin = margin - depth + offset[place]
        result = lax.slice_in_dim(result, begin, begin + inner + 2 * depth, axis=dim)
    return result


def diagonal_field(padded, margin, depth):
    total = window(padded[0], margin, depth, (0, 0, 0))
    total = total + jnp.sum(window(padded[1:], margin, depth, (0, 0, 0)), axis=0)
    for index, offset in enumerate(FORWARD):
        back = (-offset[0], -offset[1], -offset[2])
        total = total + window(padded[index + 1], margin, depth, back)
    return total


def operate(field, fmargin, padded, smargin, diag, depth):
    result = diag[None] * window(field, fmargin, depth, (0, 0, 0))
    for index, offset in enumerate(FORWARD):
        back = (-offset[0], -offset[1], -offset[2])
        ahead_w = window(padded[index + 1], smargin, depth, (0, 0, 0))
        behind_w = window(padded[index + 1], smargin, depth, back)
        result = result - ahead_w[None] * window(field, fmargin, depth, offset)
        result = result - behind_w[None] * window(field, fmargin, depth, back)
    return result


def gram(left, right):
    flat_l = left.reshape(left.shape[0], -1)
    flat_r = right.reshape(right.shape[0], -1)
    return lax.dot_general(
        flat_l,
        flat_r,
        (((1,), (1,)), ((), ())),
        precision=lax.Precision.HIGHEST,
        preferred_element_type=jnp.float32,
    )


def combine(coef, field):
    return jnp.einsum("ij,ixyz->jxyz", coef, field, precision=lax.Precision.HIGHEST)


def small_dot(left, right):
    return jnp.dot(left, right, precision=lax.Precision.HIGHEST)


def solve_spd(matrix, right):
    factor = jnp.linalg.cholesky(matrix)
    return jax.scipy.linalg.cho_solve((factor, True), right)


def joint_sum(residual, direction, image):
    parts = (
        gram(residual, residual),
        gram(direction, image),
        gram(image, residual),
        gram(image, image),
    )
    return lax.psum((parts[0], parts[1], parts[2], parts[3]), ("gx", "gy", "gz"))


def shards(rhs, stencil):
    padded = with_halo(stencil, (("gx", 1), ("gy", 2), ("gz", 3)), 1)
    smargin = 1
    diag_full = diagonal_field(padded, 1, 0)
    direction = rhs
    dmargin = 0
    residual = direction
    rmargin = dmargin
    solution = jnp.zeros_like(rhs)
    norm_now = None
    for step in range(ITERS):
        field = with_halo(direction, (("gx", 1), ("gy", 2), ("gz", 3)), 1)
        fmargin = 1
        depth = 0
        image = operate(field, fmargin, padded, smargin, diag_full, depth)
        dir_here = window(field, fmargin, depth, (0, 0, 0))
        res_here = window(residual, rmargin, depth, (0, 0, 0))
        dir_core = window(dir_here, depth, 0, (0, 0, 0))
        res_core = window(res_here, depth, 0, (0, 0, 0))
        img_core = window(image, depth, 0, (0, 0, 0))
        norm_now, curve, cross, square = joint_sum(res_core, dir_core, img_core)
        alpha = solve_spd(curve, norm_now)
        solution = solution + combine(alpha, dir_core)
        res_here = res_here - combine(alpha, image)
        if step + 1 < ITERS:
            norm_next = (
                norm_now
                - small_dot(alpha.T, cross)
                - small_dot(cross.T, alpha)
                + small_dot(alpha.T, small_dot(square, alpha))
            )
            beta = solve_spd(norm_now, norm_next)
            direction = res_here + combine(beta, dir_here)
            norm_now = norm_next
        residual = res_here
        rmargin = depth
    return (solution, window(residual, rmargin, 0, (0, 0, 0)))


def solution(mesh):
    in_specs = (P(None, "gx", "gy", "gz"), P(None, "gx", "gy", "gz"))
    out_specs = (P(None, "gx", "gy", "gz"), P(None, "gx", "gy", "gz"))
    return jax.shard_map(shards, mesh=mesh, in_specs=in_specs, out_specs=out_specs, check_vma=False)
```

profile of v0, /device:TPU:0, one launch (start us, length us, event | category | flops | bytes accessed | tf_op | source)
XLA Modules:
  0.0 386.3 jit_solution(13203145947799155079)
XLA Ops:
  4.1 4.9 %collective-permute-start.6 = (f32[8,1,32,128]{3,0,2,1:T(8,128)S(1)}, f32[8,1,32,128]{3,0,2,1:T(8,128)S(1)}, u32[]{:S(2)}, u32[]{:S(2)}) collective-permute-start(f32[8,1,32,128]{3,0,2,1:T(8,128)S(1)} %get-tuple-element.64), channel_id=1, source_target_pairs={{0,8},{8,16},{16,24},{1,9},{9,17},{17,25},{2,10},{10,18},{18,26},{... | collective-permute-start | bytes 393224 | tf_op jit(solution)/shard_map/ppermute | solution.py:20
  18.4 9.2 %collective-permute-done.7 = f32[8,1,32,128]{3,0,2,1:T(8,128)S(1)} collective-permute-done((f32[8,1,32,128]{3,0,2,1:T(8,128)S(1)}, f32[8,1,32,128]{3,0,2,1:T(8,128)S(1)}, u32[]{:S(2)}, u32[]{:S(2)}) %collective-permute-start.7) | collective-permute-done | bytes 131104 | tf_op jit(solution)/shard_map/ppermute | solution.py:22
  42.3 4.5 %collective-permute-start.11 = (f32[8,18,34,1]{2,0,3,1:T(8,128)S(1)}, f32[8,18,34,1]{2,0,3,1:T(8,128)S(1)}, u32[]{:S(2)}, u32[]{:S(2)}) collective-permute-start(f32[8,18,34,1]{2,0,3,1:T(8,128)S(1)} %copy.176), channel_id=1, source_target_pairs={{0,1},{1,2},{2,3},{4,5},{5,6},{6,7},{8,9},{9,10},{10,11},{12,13},{... | collective-permute-start | bytes 58760 | tf_op jit(solution)/shard_map/ppermute | solution.py:20
  54.8 5.5 %convolution_bitcast_fusion.5 = f32[8,8]{0,1:T(8,128)} fusion(f32[8,16,32,128]{3,2,1,0:T(8,128)S(1)} %copy-done), kind=kOutput, calls=%fused_computation.145 | convolution fusion | flops 50331648 | bytes 2097408 | tf_op jit(solution)/shard_map/dot_general | solution.py:62
  68.6 5.6 %fusion.103 = (f32[14,18,34,1]{3,2,1,0:T(8,128)}, f32[14,18,34,1]{3,2,1,0:T(8,128)}) fusion(f32[14,18,34,128]{3,2,1,0:T(8,128)S(1)} %pad_maximum_fusion.1), kind=kLoop, calls=%fused_computation.230 | loop fusion | bytes 137088 | tf_op jit(solution)/shard_map/slice | solution.py:17
  74.2 3.9 %copy.164 = f32[14,18,34,1]{2,0,3,1:T(8,128)S(1)} copy(f32[14,18,34,1]{3,2,1,0:T(8,128)} %get-tuple-element.41) | data formatting | bytes 68544 | tf_op jit(solution)/shard_map/slice | solution.py:17
  81.7 3.9 %copy.165 = f32[14,18,34,1]{2,0,3,1:T(8,128)S(1)} copy(f32[14,18,34,1]{3,2,1,0:T(8,128)} %get-tuple-element.42) | data formatting | bytes 68544 | tf_op jit(solution)/shard_map/slice | solution.py:16
  87.2 8.0 %pad_maximum_fusion.2 = (f32[8,18,34,129]{3,0,2,1:T(8,128)}, f32[8,18,34,129]{3,0,2,1:T(8,128)}) fusion(f32[8,18,34,1]{3,0,2,1:T(8,128)} %copy.175, f32[8,18,1,128]{3,0,2,1:T(8,128)S(1)} %collective-permute-done.9, f32[8,18,32,128]{3,0,2,1:T(8,128)} %copy-done.4, f32[8,18,1,128]{3,0,2,1:T(8,128)S(1)} %collective-permute-done.8, f32[8,18,34,1]{3,0,2,1:T(8,128)} %copy.177), kind=kLoop, calls=%fused_computation.2 | loop fusion | flops 3789504 | bytes 7598592 | tf_op jit(solution)/shard_map/concatenate | solution.py:18
  102.2 13.3 %pad_maximum_fusion = f32[14,18,34,130]{3,2,1,0:T(8,128)} fusion(f32[14,18,34,1]{3,2,1,0:T(8,128)} %copy.167, f32[14,18,1,128]{3,2,1,0:T(1,128)S(1)} %copy.163, f32[14,18,32,128]{3,2,1,0:T(8,128)} %copy-done.5, f32[14,18,1,128]{3,2,1,0:T(1,128)S(1)} %copy.162, f32[14,18,34,1]{3,2,1,0:T(8,128)} %copy.166), kind=kLoop, calls=%fused_computation | loop fusion | flops 4455360 | bytes 8910720 | tf_op jit(solution)/shard_map/concatenate | solution.py:18
  115.5 8.0 %slice_bitcast_fusion.13 = (f32[16,34,130]{2,1,0:T(8,128)}, f32[1,16,34,130]{3,2,1,0:T(8,128)S(1)}, f32[1,16,34,130]{3,2,1,0:T(8,128)S(1)}, f32[1,16,34,130]{3,2...) fusion(f32[14,18,34,130]{3,2,1,0:T(8,128)} %pad_maximum_fusion), kind=kLoop, calls=%fused_computation.159 | loop fusion | bytes 10749440 | tf_op jit(solution)/shard_map/slice | solution.py:35
  146.1 31.7 %fusion.17 = f32[8,16,32,128]{3,0,2,1:T(8,128)} fusion(f32[8,18,32,128]{3,0,2,1:T(8,128)} %copy-done.4, f32[8,18,1,128]{3,0,2,1:T(8,128)S(1)} %collective-permute-done.8, f32[8,18,1,128]{3,0,2,1:T(8,128)S(1)} %collective-permute-done.9, f32[8,18,34,129]{3,0,2,1:T(8,128)} %get-tuple-element.52, f32[8,18,34,129]{3,0,2,1:T(8,128)} %get-tuple-element.51, ...), kind=kLoop, calls=%fused_computation.36 | loop fusion | flops 31981568 | bytes 51789824 | tf_op jit(solution)/shard_map/sub | solution.py:55
  177.8 6.7 %fusion.100 = f32[8,8,1,1]{1,0,3,2:T(8,128)S(1)} fusion(f32[8,16,32,128]{3,0,2,1:T(8,128)} %fusion.17, f32[8,16,32,128]{3,2,1,0:T(8,128)S(1)} %copy-done), kind=kOutput, calls=%fused_computation.227 | convolution fusion | flops 50331648 | bytes 4194560 | tf_op jit(solution)/shard_map/dot_general | solution.py:62
  184.6 4.7 %convolution_bitcast_fusion.4 = f32[8,8]{1,0:T(8,128)S(1)} fusion(f32[8,16,32,128]{3,0,2,1:T(8,128)S(1)} %copy-done.2), kind=kOutput, calls=%fused_computation.142 | convolution fusion | flops 50331648 | bytes 2097408 | tf_op jit(solution)/shard_map/dot_general | solution.py:62
  189.3 40.9 %all-reduce.1 = (f32[8,8]{0,1:T(8,128)S(1)}, f32[8,8]{0,1:T(8,128)S(1)}, f32[8,8]{1,0:T(8,128)S(1)}, f32[8,8]{1,0:T(8,128)S(1)}) all-reduce(f32[8,8]{0,1:T(8,128)S(1)} %copy-done.26, f32[8,8]{0,1:T(8,128)S(1)} %bitcast.147, f32[8,8]{1,0:T(8,128)S(1)} %bitcast.148, ...), channel_id=1, replica_groups=mesh['gx'=4,'gy'=2,'gz'=4] {'gx','gy','gz'}, use_global_device_ids=true, to_apply=%region_4.6 | all-reduce | flops 256 | bytes 2048 | tf_op jit(solution)/shard_map/psum | solution.py:91
  236.0 4.7 %convolution_subtract_fusion.1 = f32[8,16,32,128]{3,0,2,1:T(8,128)S(1)} fusion(f32[8,16,32,128]{3,0,2,1:T(8,128)} %fusion.17, f32[8,8]{1,0:T(8,128)S(1)} %fusion.90, f32[8,16,32,128]{3,2,1,0:T(8,128)S(1)} %copy-done), kind=kOutput, calls=%fused_computation.136 | convolution fusion | flops 50855936 | bytes 6291712 | tf_op jit(solution)/shard_map/ij,ixyz->jxyz/dot_general | solution.py:72
  244.8 4.2 %collective-permute-start.12 = (f32[8,1,32,128]{3,0,2,1:T(8,128)S(1)}, f32[8,1,32,128]{3,0,2,1:T(8,128)S(1)}, u32[]{:S(2)}, u32[]{:S(2)}) collective-permute-start(f32[8,1,32,128]{3,0,2,1:T(8,128)S(1)} %get-tuple-element.61), channel_id=1, source_target_pairs={{0,8},{8,16},{16,24},{1,9},{9,17},{17,25},{2,10},{10,18},{18,26},{... | collective-permute-start | bytes 393224 | tf_op jit(solution)/shard_map/ppermute | solution.py:20
  250.3 4.2 %fusion.95 = f32[8,16,32,128]{3,0,2,1:T(8,128)} fusion(f32[8,8]{1,0:T(8,128)S(1)} %fusion.90, f32[8,16,32,128]{3,2,1,0:T(8,128)S(1)} %copy-done.1), kind=kOutput, calls=%fused_computation.213 | convolution fusion | flops 50331648 | bytes 4194560 | tf_op jit(solution)/shard_map/ij,ixyz->jxyz/dot_general | solution.py:72
  258.7 5.3 %convolution_bitcast_fusion.1 = f32[8,8]{1,0:T(8,128)} fusion(f32[8,16,32,128]{3,0,2,1:T(8,128)S(1)} %convolution_subtract_fusion.1), kind=kOutput, calls=%fused_computation.138 | convolution fusion | flops 50331648 | bytes 2097408 | tf_op jit(solution)/shard_map/dot_general | solution.py:62
  275.5 5.2 %collective-permute-start.17 = (f32[8,18,34,1]{2,0,3,1:T(8,128)}, f32[8,18,34,1]{2,0,3,1:T(8,128)}, u32[]{:S(2)}, u32[]{:S(2)}) collective-permute-start(f32[8,18,34,1]{2,0,3,1:T(8,128)} %copy.217), channel_id=1, source_target_pairs={{0,1},{1,2},{2,3},{4,5},{5,6},{6,7},{8,9},{9,10},{10,11},{12,13},{... | collective-permute-start | bytes 58760 | tf_op jit(solution)/shard_map/ppermute | solution.py:20
  290.0 7.8 %pad_maximum_fusion.3 = (f32[8,18,34,129]{3,0,2,1:T(8,128)}, f32[8,18,34,129]{3,0,2,1:T(8,128)}) fusion(f32[8,18,34,1]{3,0,2,1:T(8,128)} %copy.216, f32[8,18,1,128]{3,0,2,1:T(8,128)S(1)} %collective-permute-done.15, f32[8,1,32,128]{3,0,2,1:T(8,128)S(1)} %collective-permute-done.13, f32[8,16,32,128]{3,0,2,1:T(8,128)S(1)} %convolution_add_fusion.1, ...), kind=kLoop, calls=%fused_computation.4 | loop fusion | flops 6315840 | bytes 7598592 | tf_op jit(solution)/shard_map/concatenate | solution.py:18
  297.8 29.8 %fusion.30 = f32[8,16,32,128]{3,0,2,1:T(8,128)} fusion(f32[8,18,34,129]{3,0,2,1:T(8,128)} %get-tuple-element.48, f32[8,18,34,129]{3,0,2,1:T(8,128)} %get-tuple-element.47, f32[8,18,33,128]{3,0,2,1:T(8,128)} %get-tuple-element.56, f32[8,18,33,128]{3,0,2,1:T(8,128)} %get-tuple-element.55, f32[8,16,32,128]{3,0,2,1:T(8,128)S(1)} %convolution_add_fusion.1, ...), kind=kLoop, calls=%fused_computation.50 | loop fusion | flops 28835840 | bytes 61865984 | tf_op jit(solution)/shard_map/sub | solution.py:55
  327.6 6.2 %convolution_bitcast_fusion.2 = f32[8,8]{0,1:T(8,128)S(1)} fusion(f32[8,16,32,128]{3,0,2,1:T(8,128)S(1)} %convolution_add_fusion.1, f32[8,16,32,128]{3,0,2,1:T(8,128)} %fusion.30), kind=kOutput, calls=%fused_computation.139 | convolution fusion | flops 50331648 | bytes 4194560 | tf_op jit(solution)/shard_map/dot_general | solution.py:62
  333.8 38.9 %all-reduce = (f32[8,8]{1,0:T(8,128)S(1)}, f32[8,8]{0,1:T(8,128)S(1)}) all-reduce(f32[8,8]{1,0:T(8,128)S(1)} %copy-done.25, f32[8,8]{0,1:T(8,128)S(1)} %convolution_bitcast_fusion.2), channel_id=1, replica_groups=mesh['gx'=4,'gy'=2,'gz'=4] {'gx','gy','gz'}, use_global_device_ids=true, to_apply=%region_8.11 | all-reduce | flops 128 | bytes 1024 | tf_op jit(solution)/shard_map/psum | solution.py:91
  375.9 4.1 %convolution_subtract_fusion = f32[8,16,32,128]{3,0,2,1:T(8,128)S(1)} fusion(f32[8,16,32,128]{3,0,2,1:T(8,128)} %copy-done.3, f32[8,8,1,1]{0,1,3,2:T(8,128)S(1)} %convolution_bitcast_fusion, f32[8,16,32,128]{3,0,2,1:T(8,128)} %fusion.30), kind=kOutput, calls=%fused_computation.133 | convolution fusion | flops 50855936 | bytes 6291712 | tf_op jit(solution)/shard_map/ij,ixyz->jxyz/dot_general | solution.py:72
  (189 shorter events, 123.2 us)
Async XLA Ops:
  0.6 16.1 %copy-start = (f32[8,16,32,128]{3,2,1,0:T(8,128)S(1)}, f32[8,16,32,128]{3,2,1,0:T(8,128)}, u32[]{:S(2)}) copy-start(f32[8,16,32,128]{3,2,1,0:T(8,128)} %param.5) | copy-start | bytes 6291460
  4.0 12.0 %copy-start.7 = (f32[8,16,32,128]{3,0,2,1:T(8,128)}, f32[8,16,32,128]{3,0,2,1:T(8,128)S(1)}, u32[]{:S(2)}) copy-start(f32[8,16,32,128]{3,0,2,1:T(8,128)S(1)} %copy.170) | copy-start | bytes 6291460
  4.1 12.0 %collective-permute-start.6 = (f32[8,1,32,128]{3,0,2,1:T(8,128)S(1)}, f32[8,1,32,128]{3,0,2,1:T(8,128)S(1)}, u32[]{:S(2)}, u32[]{:S(2)}) collective-permute-start(f32[8,1,32,128]{3,0,2,1:T(8,128)S(1)} %get-tuple-element.64), channel_id=1, source_target_pairs={{0,8},{8,16},{16,24},{1,9},{9,17},{17,25},{2,10},{10,18},{18,26},{... | collective-permute-start | bytes 393224 | tf_op jit(solution)/shard_map/ppermute | solution.py:20
  10.0 36.8 %collective-permute-start = (f32[14,1,32,128]{3,2,1,0:T(8,128)S(1)}, f32[14,1,32,128]{3,2,1,0:T(8,128)S(1)}, u32[]{:S(2)}, u32[]{:S(2)}) collective-permute-start(f32[14,1,32,128]{3,2,1,0:T(8,128)S(1)} %get-tuple-element.46), channel_id=1, source_target_pairs={{0,8},{8,16},{16,24},{1,9},{9,17},{17,25},{2,10},{10,18},{18,26},{... | collective-permute-start | bytes 688136 | tf_op jit(solution)/shard_map/ppermute | solution.py:20
  13.5 35.9 %collective-permute-start.1 = (f32[14,1,32,128]{3,2,1,0:T(8,128)S(1)}, f32[14,1,32,128]{3,2,1,0:T(8,128)S(1)}, u32[]{:S(2)}, u32[]{:S(2)}) collective-permute-start(f32[14,1,32,128]{3,2,1,0:T(8,128)S(1)} %get-tuple-element.45), channel_id=1, source_target_pairs={{8,0},{16,8},{24,16},{9,1},{17,9},{25,17},{10,2},{18,10},{26,18},{... | collective-permute-start | bytes 688136 | tf_op jit(solution)/shard_map/ppermute | solution.py:22
  14.8 12.9 %collective-permute-start.7 = (f32[8,1,32,128]{3,0,2,1:T(8,128)S(1)}, f32[8,1,32,128]{3,0,2,1:T(8,128)S(1)}, u32[]{:S(2)}, u32[]{:S(2)}) collective-permute-start(f32[8,1,32,128]{3,0,2,1:T(8,128)S(1)} %get-tuple-element.63), channel_id=1, source_target_pairs={{8,0},{16,8},{24,16},{9,1},{17,9},{25,17},{10,2},{18,10},{26,18},{... | collective-permute-start | bytes 393224 | tf_op jit(solution)/shard_map/ppermute | solution.py:22
  16.7 13.6 %copy-start.6 = (f32[14,16,32,128]{3,2,1,0:T(8,128)S(1)}, f32[14,16,32,128]{3,2,1,0:T(8,128)}, u32[]{:S(2)}) copy-start(f32[14,16,32,128]{3,2,1,0:T(8,128)} %param.6) | copy-start | bytes 11010052
  27.7 3.7 collective-permute-start.8
  29.0 3.2 collective-permute-start.9
  38.2 22.1 %collective-permute-start.10 = (f32[8,18,34,1]{2,0,3,1:T(8,128)S(1)}, f32[8,18,34,1]{2,0,3,1:T(8,128)S(1)}, u32[]{:S(2)}, u32[]{:S(2)}) collective-permute-start(f32[8,18,34,1]{2,0,3,1:T(8,128)S(1)} %copy.174), channel_id=1, source_target_pairs={{1,0},{2,1},{3,2},{5,4},{6,5},{7,6},{9,8},{10,9},{11,10},{13,12},{... | collective-permute-start | bytes 58760 | tf_op jit(solution)/shard_map/ppermute | solution.py:22
  42.3 20.7 %collective-permute-start.11 = (f32[8,18,34,1]{2,0,3,1:T(8,128)S(1)}, f32[8,18,34,1]{2,0,3,1:T(8,128)S(1)}, u32[]{:S(2)}, u32[]{:S(2)}) collective-permute-start(f32[8,18,34,1]{2,0,3,1:T(8,128)S(1)} %copy.176), channel_id=1, source_target_pairs={{0,1},{1,2},{2,3},{4,5},{5,6},{6,7},{8,9},{9,10},{10,11},{12,13},{... | collective-permute-start | bytes 58760 | tf_op jit(solution)/shard_map/ppermute | solution.py:20
  51.5 14.0 %collective-permute-start.2 = (f32[14,18,1,128]{3,0,2,1:T(8,128)S(1)}, f32[14,18,1,128]{3,0,2,1:T(8,128)S(1)}, u32[]{:S(2)}, u32[]{:S(2)}) collective-permute-start(f32[14,18,1,128]{3,0,2,1:T(8,128)S(1)} %copy.160), channel_id=1, source_target_pairs={{0,4},{1,5},{2,6},{3,7},{8,12},{9,13},{10,14},{11,15},{16,20},{17,... | collective-permute-start | bytes 387080 | tf_op jit(solution)/shard_map/ppermute | solution.py:20
  53.2 12.4 %collective-permute-start.3 = (f32[14,18,1,128]{3,0,2,1:T(8,128)S(1)}, f32[14,18,1,128]{3,0,2,1:T(8,128)S(1)}, u32[]{:S(2)}, u32[]{:S(2)}) collective-permute-start(f32[14,18,1,128]{3,0,2,1:T(8,128)S(1)} %copy.161), channel_id=1, source_target_pairs={{4,0},{5,1},{6,2},{7,3},{12,8},{13,9},{14,10},{15,11},{20,16},{21,... | collective-permute-start | bytes 387080 | tf_op jit(solution)/shard_map/ppermute | solution.py:22
  78.2 17.0 %collective-permute-start.4 = (f32[14,18,34,1]{2,0,3,1:T(8,128)S(1)}, f32[14,18,34,1]{2,0,3,1:T(8,128)S(1)}, u32[]{:S(2)}, u32[]{:S(2)}) collective-permute-start(f32[14,18,34,1]{2,0,3,1:T(8,128)S(1)} %copy.164), channel_id=1, source_target_pairs={{0,1},{1,2},{2,3},{4,5},{5,6},{6,7},{8,9},{9,10},{10,11},{12,13},{... | collective-permute-start | bytes 102824 | tf_op jit(solution)/shard_map/ppermute | solution.py:20
  85.6 13.1 %collective-permute-start.5 = (f32[14,18,34,1]{2,0,3,1:T(8,128)S(1)}, f32[14,18,34,1]{2,0,3,1:T(8,128)S(1)}, u32[]{:S(2)}, u32[]{:S(2)}) collective-permute-start(f32[14,18,34,1]{2,0,3,1:T(8,128)S(1)} %copy.165), channel_id=1, source_target_pairs={{1,0},{2,1},{3,2},{5,4},{6,5},{7,6},{9,8},{10,9},{11,10},{13,12},{... | collective-permute-start | bytes 102824 | tf_op jit(solution)/shard_map/ppermute | solution.py:22
  146.1 31.7 %copy-start.12 = (f32[16,32,128]{2,1,0:T(8,128)}, f32[16,32,128]{2,1,0:T(8,128)S(1)}, u32[]{:S(2)}) copy-start(f32[16,32,128]{2,1,0:T(8,128)S(1)} %get-tuple-element.69) | copy-start | bytes 786436
  177.8 6.7 %copy-start.2 = (f32[8,16,32,128]{3,0,2,1:T(8,128)S(1)}, f32[8,16,32,128]{3,0,2,1:T(8,128)}, u32[]{:S(2)}) copy-start(f32[8,16,32,128]{3,0,2,1:T(8,128)} %fusion.17) | copy-start | bytes 6291460
  240.7 18.0 %copy-start.3 = (f32[8,16,32,128]{3,0,2,1:T(8,128)}, f32[8,16,32,128]{3,0,2,1:T(8,128)S(1)}, u32[]{:S(2)}) copy-start(f32[8,16,32,128]{3,0,2,1:T(8,128)S(1)} %convolution_subtract_fusion.1) | copy-start | bytes 6291460
  244.8 9.7 %collective-permute-start.12 = (f32[8,1,32,128]{3,0,2,1:T(8,128)S(1)}, f32[8,1,32,128]{3,0,2,1:T(8,128)S(1)}, u32[]{:S(2)}, u32[]{:S(2)}) collective-permute-start(f32[8,1,32,128]{3,0,2,1:T(8,128)S(1)} %get-tuple-element.61), channel_id=1, source_target_pairs={{0,8},{8,16},{16,24},{1,9},{9,17},{17,25},{2,10},{10,18},{18,26},{... | collective-permute-start | bytes 393224 | tf_op jit(solution)/shard_map/ppermute | solution.py:20
  249.0 6.9 %collective-permute-start.13 = (f32[8,1,32,128]{3,0,2,1:T(8,128)S(1)}, f32[8,1,32,128]{3,0,2,1:T(8,128)S(1)}, u32[]{:S(2)}, u32[]{:S(2)}) collective-permute-start(f32[8,1,32,128]{3,0,2,1:T(8,128)S(1)} %get-tuple-element.62), channel_id=1, source_target_pairs={{8,0},{16,8},{24,16},{9,1},{17,9},{25,17},{10,2},{18,10},{26,18},{... | collective-permute-start | bytes 393224 | tf_op jit(solution)/shard_map/ppermute | solution.py:22
  255.9 8.1 %collective-permute-start.14 = (f32[8,18,1,128]{3,0,2,1:T(8,128)S(1)}, f32[8,18,1,128]{3,0,2,1:T(8,128)S(1)}, u32[]{:S(2)}, u32[]{:S(2)}) collective-permute-start(f32[8,18,1,128]{3,0,2,1:T(8,128)S(1)} %get-tuple-element.57), channel_id=1, source_target_pairs={{0,4},{1,5},{2,6},{3,7},{8,12},{9,13},{10,14},{11,15},{16,20},{17,... | collective-permute-start | bytes 221192 | tf_op jit(solution)/shard_map/ppermute | solution.py:20
  257.2 6.8 %collective-permute-start.15 = (f32[8,18,1,128]{3,0,2,1:T(8,128)S(1)}, f32[8,18,1,128]{3,0,2,1:T(8,128)S(1)}, u32[]{:S(2)}, u32[]{:S(2)}) collective-permute-start(f32[8,18,1,128]{3,0,2,1:T(8,128)S(1)} %get-tuple-element.58), channel_id=1, source_target_pairs={{4,0},{5,1},{6,2},{7,3},{12,8},{13,9},{14,10},{15,11},{20,16},{21,... | collective-permute-start | bytes 221192 | tf_op jit(solution)/shard_map/ppermute | solution.py:22
  270.7 12.4 %collective-permute-start.16 = (f32[8,18,34,1]{2,0,3,1:T(8,128)}, f32[8,18,34,1]{2,0,3,1:T(8,128)}, u32[]{:S(2)}, u32[]{:S(2)}) collective-permute-start(f32[8,18,34,1]{2,0,3,1:T(8,128)} %copy.215), channel_id=1, source_target_pairs={{1,0},{2,1},{3,2},{5,4},{6,5},{7,6},{9,8},{10,9},{11,10},{13,12},{... | collective-permute-start | bytes 58760 | tf_op jit(solution)/shard_map/ppermute | solution.py:22
  275.5 11.1 %collective-permute-start.17 = (f32[8,18,34,1]{2,0,3,1:T(8,128)}, f32[8,18,34,1]{2,0,3,1:T(8,128)}, u32[]{:S(2)}, u32[]{:S(2)}) collective-permute-start(f32[8,18,34,1]{2,0,3,1:T(8,128)} %copy.217), channel_id=1, source_target_pairs={{0,1},{1,2},{2,3},{4,5},{5,6},{6,7},{8,9},{9,10},{10,11},{12,13},{... | collective-permute-start | bytes 58760 | tf_op jit(solution)/shard_map/ppermute | solution.py:20
  (21 other events, 81.8 us)
where the time goes:
time: 393 us; the launch traced here: 386 us
  other arithmetic  107 us (27%)
  local copies, waits for them, and re-layouts  95.5 us (24%)
  blocking collectives  79.8 us (20%)
  matrix products  48.1 us (12%)
  starting transfers between devices  42.2 us (11%)
  waiting for transfers between devices  11.5 us (3%)
    psum x2, blocking collectives, joint_sum(): lax.psum((parts[0], parts[1], parts[2], parts[3]), ('gx', 'gy', 'gz'))  79.8 us
    sub x2, other arithmetic, operate(): result = result - behind_w[None] * window(field, fmargin, depth, back)  61.5 us
    concatenate x7, other arithmetic, with_halo(): jnp.concatenate([lax.ppermute(tail, axis, [(i, (i + 1) % count) for i in...  34.7 us
    ppermute x9, starting transfers between devices, with_halo(): lax.ppermute(tail, axis, [(i, (i + 1) % count) for i in range(ends)])  30 us
    dot_general x5, matrix products, gram(): lax.dot_general(flat_l, flat_r, (((1,), (1,)), ((), ())), precision=lax.P...  28.4 us
    slice x35, local copies, waits for them, and re-layouts, window(): lax.slice_in_dim(result, begin, begin + inner + 2 * depth, axis=dim)  28.3 us
    dot_general x5, matrix products, combine(): jnp.einsum('ij,ixyz->jxyz', coef, field, precision=lax.Precision.HIGHEST)  17.8 us
    slice x9, local copies, waits for them, and re-layouts, with_halo(): head = lax.slice_in_dim(cells, 0, width, axis=dim)  17.4 us
  transfers between devices with their start and end apart: 18, of which 3 were waited for; matrix products, arithmetic and copies ran while one was open for 16% of the time, Pallas kernels for 0%

commit v1 on v0

--- a/solution.py
+++ b/solution.py
@@ -88,7 +88,7 @@
         gram(image, residual),
         gram(image, image),
     )
-    return lax.psum((parts[0], parts[1], parts[2], parts[3]), ("gx", "gy", "gz"))
+    return lax.psum(lax.psum((parts[0], parts[1], parts[2], parts[3]), ("gy", "gz")), "gx")
 
 
 def shards(rhs, stencil):

time: 393 us -> 380 us (0.967)
  blocking collectives: 79.8 us -> 68.7 us
    psum x2 -> x4, blocking collectives: 79.8 us -> 68.7 us  [the longest x2 43.8 us: joint_sum(): lax.psum((parts[0], parts[1], parts[2], parts[3]), ('gy', 'gz'))]
where the time goes in v1:
time: 380 us; the launch traced here: 373 us
  other arithmetic  106 us (28%)
  local copies, waits for them, and re-layouts  95.7 us (25%)
  blocking collectives  68.7 us (18%)
  matrix products  48.1 us (13%)
  starting transfers between devices  41.3 us (11%)
  waiting for transfers between devices  11.6 us (3%)
    sub x2, other arithmetic, operate(): result = result - behind_w[None] * window(field, fmargin, depth, back)  60.2 us
    psum x2, blocking collectives, joint_sum(): lax.psum((parts[0], parts[1], parts[2], parts[3]), ('gy', 'gz'))  43.8 us
    concatenate x7, other arithmetic, with_halo(): jnp.concatenate([lax.ppermute(tail, axis, [(i, (i + 1) % count) for i in...  34.6 us
    ppermute x9, starting transfers between devices, with_halo(): lax.ppermute(tail, axis, [(i, (i + 1) % count) for i in range(ends)])  28.5 us
    slice x35, local copies, waits for them, and re-layouts, window(): lax.slice_in_dim(result, begin, begin + inner + 2 * depth, axis=dim)  28.4 us
    dot_general x5, matrix products, gram(): lax.dot_general(flat_l, flat_r, (((1,), (1,)), ((), ())), precision=lax.P...  28.4 us
    psum x2, blocking collectives, joint_sum(): lax.psum(lax.psum((parts[0], parts[1], parts[2], parts[3]), ('gy', 'gz'))...  24.9 us
    dot_general x5, matrix products, combine(): jnp.einsum('ij,ixyz->jxyz', coef, field, precision=lax.Precision.HIGHEST)  17.8 us
  transfers between devices with their start and end apart: 18, of which 3 were waited for; matrix products, arithmetic and copies ran while one was open for 16% of the time, Pallas kernels for 0%

profile of v1, /device:TPU:0, one launch (start us, length us, event | category | flops | bytes accessed | tf_op | source)
XLA Modules:
  0.0 372.9 jit_solution(9153637627434092762)
XLA Ops:
  4.1 4.9 %collective-permute-start.6 = (f32[8,1,32,128]{3,0,2,1:T(8,128)S(1)}, f32[8,1,32,128]{3,0,2,1:T(8,128)S(1)}, u32[]{:S(2)}, u32[]{:S(2)}) collective-permute-start(f32[8,1,32,128]{3,0,2,1:T(8,128)S(1)} %get-tuple-element.70), channel_id=1, source_target_pairs={{0,8},{8,16},{16,24},{1,9},{9,17},{17,25},{2,10},{10,18},{18,26},{... | collective-permute-start | bytes 393224 | tf_op jit(solution)/shard_map/ppermute | solution.py:20
  18.4 9.2 %collective-permute-done.7 = f32[8,1,32,128]{3,0,2,1:T(8,128)S(1)} collective-permute-done((f32[8,1,32,128]{3,0,2,1:T(8,128)S(1)}, f32[8,1,32,128]{3,0,2,1:T(8,128)S(1)}, u32[]{:S(2)}, u32[]{:S(2)}) %collective-permute-start.7) | collective-permute-done | bytes 131104 | tf_op jit(solution)/shard_map/ppermute | solution.py:22
  42.3 4.5 %collective-permute-start.11 = (f32[8,18,34,1]{2,0,3,1:T(8,128)S(1)}, f32[8,18,34,1]{2,0,3,1:T(8,128)S(1)}, u32[]{:S(2)}, u32[]{:S(2)}) collective-permute-start(f32[8,18,34,1]{2,0,3,1:T(8,128)S(1)} %copy.176), channel_id=1, source_target_pairs={{0,1},{1,2},{2,3},{4,5},{5,6},{6,7},{8,9},{9,10},{10,11},{12,13},{... | collective-permute-start | bytes 58760 | tf_op jit(solution)/shard_map/ppermute | solution.py:20
  54.9 5.5 %convolution_bitcast_fusion.5 = f32[8,8]{0,1:T(8,128)} fusion(f32[8,16,32,128]{3,2,1,0:T(8,128)S(1)} %copy-done), kind=kOutput, calls=%fused_computation.145 | convolution fusion | flops 50331648 | bytes 2097408 | tf_op jit(solution)/shard_map/dot_general | solution.py:62
  68.7 5.6 %fusion.103 = (f32[14,18,34,1]{3,2,1,0:T(8,128)}, f32[14,18,34,1]{3,2,1,0:T(8,128)}) fusion(f32[14,18,34,128]{3,2,1,0:T(8,128)S(1)} %pad_maximum_fusion.1), kind=kLoop, calls=%fused_computation.230 | loop fusion | bytes 137088 | tf_op jit(solution)/shard_map/slice | solution.py:17
  81.8 3.9 %copy.165 = f32[14,18,34,1]{2,0,3,1:T(8,128)S(1)} copy(f32[14,18,34,1]{3,2,1,0:T(8,128)} %get-tuple-element.48) | data formatting | bytes 68544 | tf_op jit(solution)/shard_map/slice | solution.py:16
  87.5 7.9 %pad_maximum_fusion.2 = (f32[8,18,34,129]{3,0,2,1:T(8,128)}, f32[8,18,34,129]{3,0,2,1:T(8,128)}) fusion(f32[8,18,34,1]{3,0,2,1:T(8,128)} %copy.175, f32[8,18,1,128]{3,0,2,1:T(8,128)S(1)} %collective-permute-done.9, f32[8,18,32,128]{3,0,2,1:T(8,128)} %copy-done.4, f32[8,18,1,128]{3,0,2,1:T(8,128)S(1)} %collective-permute-done.8, f32[8,18,34,1]{3,0,2,1:T(8,128)} %copy.177), kind=kLoop, calls=%fused_computation.2 | loop fusion | flops 3789504 | bytes 7598592 | tf_op jit(solution)/shard_map/concatenate | solution.py:18
  102.6 13.2 %pad_maximum_fusion = f32[14,18,34,130]{3,2,1,0:T(8,128)} fusion(f32[14,18,34,1]{3,2,1,0:T(8,128)} %copy.167, f32[14,18,1,128]{3,2,1,0:T(1,128)S(1)} %copy.163, f32[14,18,32,128]{3,2,1,0:T(8,128)} %copy-done.5, f32[14,18,1,128]{3,2,1,0:T(1,128)S(1)} %copy.162, f32[14,18,34,1]{3,2,1,0:T(8,128)} %copy.166), kind=kLoop, calls=%fused_computation | loop fusion | flops 4455360 | bytes 8910720 | tf_op jit(solution)/shard_map/concatenate | solution.py:18
  115.8 8.1 %slice_bitcast_fusion.13 = (f32[16,34,130]{2,1,0:T(8,128)}, f32[1,16,34,130]{3,2,1,0:T(8,128)S(1)}, f32[1,16,34,130]{3,2,1,0:T(8,128)S(1)}, f32[1,16,34,130]{3,2...) fusion(f32[14,18,34,130]{3,2,1,0:T(8,128)} %pad_maximum_fusion), kind=kLoop, calls=%fused_computation.159 | loop fusion | bytes 10749440 | tf_op jit(solution)/shard_map/slice | solution.py:35
  146.6 31.0 %fusion.17 = f32[8,16,32,128]{3,0,2,1:T(8,128)} fusion(f32[8,18,32,128]{3,0,2,1:T(8,128)} %copy-done.4, f32[8,18,1,128]{3,0,2,1:T(8,128)S(1)} %collective-permute-done.8, f32[8,18,1,128]{3,0,2,1:T(8,128)S(1)} %collective-permute-done.9, f32[8,18,34,129]{3,0,2,1:T(8,128)} %get-tuple-element.58, f32[8,18,34,129]{3,0,2,1:T(8,128)} %get-tuple-element.57, ...), kind=kLoop, calls=%fused_computation.36 | loop fusion | flops 31981568 | bytes 51789824 | tf_op jit(solution)/shard_map/sub | solution.py:55
  177.7 6.7 %fusion.100 = f32[8,8,1,1]{1,0,3,2:T(8,128)S(1)} fusion(f32[8,16,32,128]{3,0,2,1:T(8,128)} %fusion.17, f32[8,16,32,128]{3,2,1,0:T(8,128)S(1)} %copy-done), kind=kOutput, calls=%fused_computation.227 | convolution fusion | flops 50331648 | bytes 4194560 | tf_op jit(solution)/shard_map/dot_general | solution.py:62
  184.4 4.7 %convolution_bitcast_fusion.4 = f32[8,8]{1,0:T(8,128)S(1)} fusion(f32[8,16,32,128]{3,0,2,1:T(8,128)S(1)} %copy-done.2), kind=kOutput, calls=%fused_computation.142 | convolution fusion | flops 50331648 | bytes 2097408 | tf_op jit(solution)/shard_map/dot_general | solution.py:62
  189.1 29.5 %all-reduce.1 = (f32[8,8]{0,1:T(8,128)S(1)}, f32[8,8]{0,1:T(8,128)S(1)}, f32[8,8]{1,0:T(8,128)S(1)}, f32[8,8]{1,0:T(8,128)S(1)}) all-reduce(f32[8,8]{0,1:T(8,128)S(1)} %copy-done.26, f32[8,8]{0,1:T(8,128)S(1)} %bitcast.147, f32[8,8]{1,0:T(8,128)S(1)} %bitcast.148, ...), channel_id=1, replica_groups=mesh['gx'=4,'gy'=2,'gz'=4] {'gy','gz'}, use_global_device_ids=true, to_apply=%region_5.7 | all-reduce | flops 256 | bytes 2048 | tf_op jit(solution)/shard_map/psum | solution.py:91
  218.6 14.2 %all-reduce.3 = (f32[8,8]{0,1:T(8,128)S(1)}, f32[8,8]{0,1:T(8,128)S(1)}, f32[8,8]{1,0:T(8,128)S(1)}, f32[8,8]{1,0:T(8,128)S(1)}) all-reduce(f32[8,8]{0,1:T(8,128)S(1)} %get-tuple-element.14, f32[8,8]{0,1:T(8,128)S(1)} %get-tuple-element.15, f32[8,8]{1,0:T(8,128)S(1)} %get-tuple-element.16, ...), channel_id=1, replica_groups=mesh['gx'=4,'gy'=2,'gz'=4] {'gx'}, use_global_device_ids=true, to_apply=%region_6.8 | all-reduce | flops 256 | bytes 2048 | tf_op jit(solution)/shard_map/psum | solution.py:91
  238.6 4.7 %convolution_subtract_fusion.1 = f32[8,16,32,128]{3,0,2,1:T(8,128)S(1)} fusion(f32[8,16,32,128]{3,0,2,1:T(8,128)} %fusion.17, f32[8,8]{1,0:T(8,128)S(1)} %fusion.90, f32[8,16,32,128]{3,2,1,0:T(8,128)S(1)} %copy-done), kind=kOutput, calls=%fused_computation.136 | convolution fusion | flops 50855936 | bytes 6291712 | tf_op jit(solution)/shard_map/ij,ixyz->jxyz/dot_general | solution.py:72
  251.5 4.2 %fusion.95 = f32[8,16,32,128]{3,0,2,1:T(8,128)} fusion(f32[8,8]{1,0:T(8,128)S(1)} %fusion.90, f32[8,16,32,128]{3,2,1,0:T(8,128)S(1)} %copy-done.1), kind=kOutput, calls=%fused_computation.213 | convolution fusion | flops 50331648 | bytes 4194560 | tf_op jit(solution)/shard_map/ij,ixyz->jxyz/dot_general | solution.py:72
  260.2 5.3 %convolution_bitcast_fusion.1 = f32[8,8]{1,0:T(8,128)} fusion(f32[8,16,32,128]{3,0,2,1:T(8,128)S(1)} %convolution_subtract_fusion.1), kind=kOutput, calls=%fused_computation.138 | convolution fusion | flops 50331648 | bytes 2097408 | tf_op jit(solution)/shard_map/dot_general | solution.py:62
  276.9 5.2 %collective-permute-start.17 = (f32[8,18,34,1]{2,0,3,1:T(8,128)}, f32[8,18,34,1]{2,0,3,1:T(8,128)}, u32[]{:S(2)}, u32[]{:S(2)}) collective-permute-start(f32[8,18,34,1]{2,0,3,1:T(8,128)} %copy.217), channel_id=1, source_target_pairs={{0,1},{1,2},{2,3},{4,5},{5,6},{6,7},{8,9},{9,10},{10,11},{12,13},{... | collective-permute-start | bytes 58760 | tf_op jit(solution)/shard_map/ppermute | solution.py:20
  291.5 7.8 %pad_maximum_fusion.3 = (f32[8,18,34,129]{3,0,2,1:T(8,128)}, f32[8,18,34,129]{3,0,2,1:T(8,128)}) fusion(f32[8,18,34,1]{3,0,2,1:T(8,128)} %copy.216, f32[8,18,1,128]{3,0,2,1:T(8,128)S(1)} %collective-permute-done.15, f32[8,1,32,128]{3,0,2,1:T(8,128)S(1)} %collective-permute-done.13, f32[8,16,32,128]{3,0,2,1:T(8,128)S(1)} %convolution_add_fusion.1, ...), kind=kLoop, calls=%fused_computation.4 | loop fusion | flops 6315840 | bytes 7598592 | tf_op jit(solution)/shard_map/concatenate | solution.py:18
  299.3 29.1 %fusion.30 = f32[8,16,32,128]{3,0,2,1:T(8,128)} fusion(f32[8,18,34,129]{3,0,2,1:T(8,128)} %get-tuple-element.54, f32[8,18,34,129]{3,0,2,1:T(8,128)} %get-tuple-element.53, f32[8,18,33,128]{3,0,2,1:T(8,128)} %get-tuple-element.62, f32[8,18,33,128]{3,0,2,1:T(8,128)} %get-tuple-element.61, f32[8,16,32,128]{3,0,2,1:T(8,128)S(1)} %convolution_add_fusion.1, ...), kind=kLoop, calls=%fused_computation.50 | loop fusion | flops 28835840 | bytes 61865984 | tf_op jit(solution)/shard_map/sub | solution.py:55
  328.4 6.2 %convolution_bitcast_fusion.2 = f32[8,8]{0,1:T(8,128)S(1)} fusion(f32[8,16,32,128]{3,0,2,1:T(8,128)S(1)} %convolution_add_fusion.1, f32[8,16,32,128]{3,0,2,1:T(8,128)} %fusion.30), kind=kOutput, calls=%fused_computation.139 | convolution fusion | flops 50331648 | bytes 4194560 | tf_op jit(solution)/shard_map/dot_general | solution.py:62
  334.7 14.3 %all-reduce = (f32[8,8]{1,0:T(8,128)S(1)}, f32[8,8]{0,1:T(8,128)S(1)}) all-reduce(f32[8,8]{1,0:T(8,128)S(1)} %copy-done.25, f32[8,8]{0,1:T(8,128)S(1)} %convolution_bitcast_fusion.2), channel_id=1, replica_groups=mesh['gx'=4,'gy'=2,'gz'=4] {'gy','gz'}, use_global_device_ids=true, to_apply=%region_13.16 | all-reduce | flops 128 | bytes 1024 | tf_op jit(solution)/shard_map/psum | solution.py:91
  348.9 10.7 %all-reduce.2 = (f32[8,8]{1,0:T(8,128)S(1)}, f32[8,8]{0,1:T(8,128)S(1)}) all-reduce(f32[8,8]{1,0:T(8,128)S(1)} %get-tuple-element.12, f32[8,8]{0,1:T(8,128)S(1)} %get-tuple-element.13), channel_id=1, replica_groups=mesh['gx'=4,'gy'=2,'gz'=4] {'gx'}, use_global_device_ids=true, to_apply=%region_14.17 | all-reduce | flops 128 | bytes 1024 | tf_op jit(solution)/shard_map/psum | solution.py:91
  362.9 4.1 %convolution_subtract_fusion = f32[8,16,32,128]{3,0,2,1:T(8,128)S(1)} fusion(f32[8,16,32,128]{3,0,2,1:T(8,128)} %copy-done.3, f32[8,8,1,1]{0,1,3,2:T(8,128)S(1)} %convolution_bitcast_fusion, f32[8,16,32,128]{3,0,2,1:T(8,128)} %fusion.30), kind=kOutput, calls=%fused_computation.133 | convolution fusion | flops 50855936 | bytes 6291712 | tf_op jit(solution)/shard_map/ij,ixyz->jxyz/dot_general | solution.py:72
  (191 shorter events, 130.7 us)
Async XLA Ops:
  0.6 16.1 %copy-start = (f32[8,16,32,128]{3,2,1,0:T(8,128)S(1)}, f32[8,16,32,128]{3,2,1,0:T(8,128)}, u32[]{:S(2)}) copy-start(f32[8,16,32,128]{3,2,1,0:T(8,128)} %param.5) | copy-start | bytes 6291460
  4.0 12.0 %copy-start.7 = (f32[8,16,32,128]{3,0,2,1:T(8,128)}, f32[8,16,32,128]{3,0,2,1:T(8,128)S(1)}, u32[]{:S(2)}) copy-start(f32[8,16,32,128]{3,0,2,1:T(8,128)S(1)} %copy.170) | copy-start | bytes 6291460
  4.1 12.0 %collective-permute-start.6 = (f32[8,1,32,128]{3,0,2,1:T(8,128)S(1)}, f32[8,1,32,128]{3,0,2,1:T(8,128)S(1)}, u32[]{:S(2)}, u32[]{:S(2)}) collective-permute-start(f32[8,1,32,128]{3,0,2,1:T(8,128)S(1)} %get-tuple-element.70), channel_id=1, source_target_pairs={{0,8},{8,16},{16,24},{1,9},{9,17},{17,25},{2,10},{10,18},{18,26},{... | collective-permute-start | bytes 393224 | tf_op jit(solution)/shard_map/ppermute | solution.py:20
  10.0 36.8 %collective-permute-start = (f32[14,1,32,128]{3,2,1,0:T(8,128)S(1)}, f32[14,1,32,128]{3,2,1,0:T(8,128)S(1)}, u32[]{:S(2)}, u32[]{:S(2)}) collective-permute-start(f32[14,1,32,128]{3,2,1,0:T(8,128)S(1)} %get-tuple-element.52), channel_id=1, source_target_pairs={{0,8},{8,16},{16,24},{1,9},{9,17},{17,25},{2,10},{10,18},{18,26},{... | collective-permute-start | bytes 688136 | tf_op jit(solution)/shard_map/ppermute | solution.py:20
  13.5 35.9 %collective-permute-start.1 = (f32[14,1,32,128]{3,2,1,0:T(8,128)S(1)}, f32[14,1,32,128]{3,2,1,0:T(8,128)S(1)}, u32[]{:S(2)}, u32[]{:S(2)}) collective-permute-start(f32[14,1,32,128]{3,2,1,0:T(8,128)S(1)} %get-tuple-element.51), channel_id=1, source_target_pairs={{8,0},{16,8},{24,16},{9,1},{17,9},{25,17},{10,2},{18,10},{26,18},{... | collective-permute-start | bytes 688136 | tf_op jit(solution)/shard_map/ppermute | solution.py:22
  14.8 12.9 %collective-permute-start.7 = (f32[8,1,32,128]{3,0,2,1:T(8,128)S(1)}, f32[8,1,32,128]{3,0,2,1:T(8,128)S(1)}, u32[]{:S(2)}, u32[]{:S(2)}) collective-permute-start(f32[8,1,32,128]{3,0,2,1:T(8,128)S(1)} %get-tuple-element.69), channel_id=1, source_target_pairs={{8,0},{16,8},{24,16},{9,1},{17,9},{25,17},{10,2},{18,10},{26,18},{... | collective-permute-start | bytes 393224 | tf_op jit(solution)/shard_map/ppermute | solution.py:22
  16.7 13.6 %copy-start.6 = (f32[14,16,32,128]{3,2,1,0:T(8,128)S(1)}, f32[14,16,32,128]{3,2,1,0:T(8,128)}, u32[]{:S(2)}) copy-start(f32[14,16,32,128]{3,2,1,0:T(8,128)} %param.6) | copy-start | bytes 11010052
  27.7 3.7 collective-permute-start.8
  29.0 3.2 collective-permute-start.9
  38.2 22.2 %collective-permute-start.10 = (f32[8,18,34,1]{2,0,3,1:T(8,128)S(1)}, f32[8,18,34,1]{2,0,3,1:T(8,128)S(1)}, u32[]{:S(2)}, u32[]{:S(2)}) collective-permute-start(f32[8,18,34,1]{2,0,3,1:T(8,128)S(1)} %copy.174), channel_id=1, source_target_pairs={{1,0},{2,1},{3,2},{5,4},{6,5},{7,6},{9,8},{10,9},{11,10},{13,12},{... | collective-permute-start | bytes 58760 | tf_op jit(solution)/shard_map/ppermute | solution.py:22
  42.3 20.8 %collective-permute-start.11 = (f32[8,18,34,1]{2,0,3,1:T(8,128)S(1)}, f32[8,18,34,1]{2,0,3,1:T(8,128)S(1)}, u32[]{:S(2)}, u32[]{:S(2)}) collective-permute-start(f32[8,18,34,1]{2,0,3,1:T(8,128)S(1)} %copy.176), channel_id=1, source_target_pairs={{0,1},{1,2},{2,3},{4,5},{5,6},{6,7},{8,9},{9,10},{10,11},{12,13},{... | collective-permute-start | bytes 58760 | tf_op jit(solution)/shard_map/ppermute | solution.py:20
  51.5 14.1 %collective-permute-start.2 = (f32[14,18,1,128]{3,0,2,1:T(8,128)S(1)}, f32[14,18,1,128]{3,0,2,1:T(8,128)S(1)}, u32[]{:S(2)}, u32[]{:S(2)}) collective-permute-start(f32[14,18,1,128]{3,0,2,1:T(8,128)S(1)} %copy.160), channel_id=1, source_target_pairs={{0,4},{1,5},{2,6},{3,7},{8,12},{9,13},{10,14},{11,15},{16,20},{17,... | collective-permute-start | bytes 387080 | tf_op jit(solution)/shard_map/ppermute | solution.py:20
  53.3 12.5 %collective-permute-start.3 = (f32[14,18,1,128]{3,0,2,1:T(8,128)S(1)}, f32[14,18,1,128]{3,0,2,1:T(8,128)S(1)}, u32[]{:S(2)}, u32[]{:S(2)}) collective-permute-start(f32[14,18,1,128]{3,0,2,1:T(8,128)S(1)} %copy.161), channel_id=1, source_target_pairs={{4,0},{5,1},{6,2},{7,3},{12,8},{13,9},{14,10},{15,11},{20,16},{21,... | collective-permute-start | bytes 387080 | tf_op jit(solution)/shard_map/ppermute | solution.py:22
  78.3 17.2 %collective-permute-start.4 = (f32[14,18,34,1]{2,0,3,1:T(8,128)S(1)}, f32[14,18,34,1]{2,0,3,1:T(8,128)S(1)}, u32[]{:S(2)}, u32[]{:S(2)}) collective-permute-start(f32[14,18,34,1]{2,0,3,1:T(8,128)S(1)} %copy.164), channel_id=1, source_target_pairs={{0,1},{1,2},{2,3},{4,5},{5,6},{6,7},{8,9},{9,10},{10,11},{12,13},{... | collective-permute-start | bytes 102824 | tf_op jit(solution)/shard_map/ppermute | solution.py:20
  85.7 13.3 %collective-permute-start.5 = (f32[14,18,34,1]{2,0,3,1:T(8,128)S(1)}, f32[14,18,34,1]{2,0,3,1:T(8,128)S(1)}, u32[]{:S(2)}, u32[]{:S(2)}) collective-permute-start(f32[14,18,34,1]{2,0,3,1:T(8,128)S(1)} %copy.165), channel_id=1, source_target_pairs={{1,0},{2,1},{3,2},{5,4},{6,5},{7,6},{9,8},{10,9},{11,10},{13,12},{... | collective-permute-start | bytes 102824 | tf_op jit(solution)/shard_map/ppermute | solution.py:22
  146.6 31.1 %copy-start.12 = (f32[16,32,128]{2,1,0:T(8,128)}, f32[16,32,128]{2,1,0:T(8,128)S(1)}, u32[]{:S(2)}) copy-start(f32[16,32,128]{2,1,0:T(8,128)S(1)} %get-tuple-element.75) | copy-start | bytes 786436
  177.7 6.7 %copy-start.2 = (f32[8,16,32,128]{3,0,2,1:T(8,128)S(1)}, f32[8,16,32,128]{3,0,2,1:T(8,128)}, u32[]{:S(2)}) copy-start(f32[8,16,32,128]{3,0,2,1:T(8,128)} %fusion.17) | copy-start | bytes 6291460
  243.4 16.8 %copy-start.3 = (f32[8,16,32,128]{3,0,2,1:T(8,128)}, f32[8,16,32,128]{3,0,2,1:T(8,128)S(1)}, u32[]{:S(2)}) copy-start(f32[8,16,32,128]{3,0,2,1:T(8,128)S(1)} %convolution_subtract_fusion.1) | copy-start | bytes 6291460
  247.5 8.2 %collective-permute-start.12 = (f32[8,1,32,128]{3,0,2,1:T(8,128)S(1)}, f32[8,1,32,128]{3,0,2,1:T(8,128)S(1)}, u32[]{:S(2)}, u32[]{:S(2)}) collective-permute-start(f32[8,1,32,128]{3,0,2,1:T(8,128)S(1)} %get-tuple-element.67), channel_id=1, source_target_pairs={{0,8},{8,16},{16,24},{1,9},{9,17},{17,25},{2,10},{10,18},{18,26},{... | collective-permute-start | bytes 393224 | tf_op jit(solution)/shard_map/ppermute | solution.py:20
  250.2 7.0 %collective-permute-start.13 = (f32[8,1,32,128]{3,0,2,1:T(8,128)S(1)}, f32[8,1,32,128]{3,0,2,1:T(8,128)S(1)}, u32[]{:S(2)}, u32[]{:S(2)}) collective-permute-start(f32[8,1,32,128]{3,0,2,1:T(8,128)S(1)} %get-tuple-element.68), channel_id=1, source_target_pairs={{8,0},{16,8},{24,16},{9,1},{17,9},{25,17},{10,2},{18,10},{26,18},{... | collective-permute-start | bytes 393224 | tf_op jit(solution)/shard_map/ppermute | solution.py:22
  257.2 8.3 %collective-permute-start.14 = (f32[8,18,1,128]{3,0,2,1:T(8,128)S(1)}, f32[8,18,1,128]{3,0,2,1:T(8,128)S(1)}, u32[]{:S(2)}, u32[]{:S(2)}) collective-permute-start(f32[8,18,1,128]{3,0,2,1:T(8,128)S(1)} %get-tuple-element.63), channel_id=1, source_target_pairs={{0,4},{1,5},{2,6},{3,7},{8,12},{9,13},{10,14},{11,15},{16,20},{17,... | collective-permute-start | bytes 221192 | tf_op jit(solution)/shard_map/ppermute | solution.py:20
  258.5 7.0 %collective-permute-start.15 = (f32[8,18,1,128]{3,0,2,1:T(8,128)S(1)}, f32[8,18,1,128]{3,0,2,1:T(8,128)S(1)}, u32[]{:S(2)}, u32[]{:S(2)}) collective-permute-start(f32[8,18,1,128]{3,0,2,1:T(8,128)S(1)} %get-tuple-element.64), channel_id=1, source_target_pairs={{4,0},{5,1},{6,2},{7,3},{12,8},{13,9},{14,10},{15,11},{20,16},{21,... | collective-permute-start | bytes 221192 | tf_op jit(solution)/shard_map/ppermute | solution.py:22
  272.2 12.4 %collective-permute-start.16 = (f32[8,18,34,1]{2,0,3,1:T(8,128)}, f32[8,18,34,1]{2,0,3,1:T(8,128)}, u32[]{:S(2)}, u32[]{:S(2)}) collective-permute-start(f32[8,18,34,1]{2,0,3,1:T(8,128)} %copy.215), channel_id=1, source_target_pairs={{1,0},{2,1},{3,2},{5,4},{6,5},{7,6},{9,8},{10,9},{11,10},{13,12},{... | collective-permute-start | bytes 58760 | tf_op jit(solution)/shard_map/ppermute | solution.py:22
  276.9 11.1 %collective-permute-start.17 = (f32[8,18,34,1]{2,0,3,1:T(8,128)}, f32[8,18,34,1]{2,0,3,1:T(8,128)}, u32[]{:S(2)}, u32[]{:S(2)}) collective-permute-start(f32[8,18,34,1]{2,0,3,1:T(8,128)} %copy.217), channel_id=1, source_target_pairs={{0,1},{1,2},{2,3},{4,5},{5,6},{6,7},{8,9},{9,10},{10,11},{12,13},{... | collective-permute-start | bytes 58760 | tf_op jit(solution)/shard_map/ppermute | solution.py:20
  (21 other events, 81.9 us)
